TPU v7x, 512 devices: a whole 4x8x8 slice. The times are simulated.
512 devices in a mesh: seq: 64 (over z, x, core), tp: 8 (over y).
Axes of the slice: x: 4, y: 8, z: 8, core: 2. Of those that a mesh axis runs over, the one named last changes fastest.
Arguments:
- hidden_in: bfloat16 [8192, 4096], P('seq', 'tp'), may hold values from -64 to 64
- span_order: int32 [64], replicated, may hold values from 0 to 63, each once
- norm_gain: bfloat16 [4096], P('tp'), may hold values from 0.099609375 to 1.8984375
- w_query: bfloat16 [4096, 4096], P('seq', 'tp'), may hold values from -0.09375 to 0.09375
- bias_query: bfloat16 [4096], P('tp'), may hold values from -14 to 14
- key_value_weight: bfloat16 [4096, 2, 1024], P('seq', None, 'tp'), may hold values from -0.09375 to 0.09375
- bias_kv: bfloat16 [2, 1024], P(None, 'tp'), may hold values from -14 to 14
- w_out: bfloat16 [4096, 4096], P('tp', 'seq'), may hold values from -0.09375 to 0.09375
- post_gain: bfloat16 [4096], P('tp'), may hold values from 0.099609375 to 1.8984375
Outputs:
- attn_out: bfloat16 [8192, 4096], P('seq', 'tp')
- normed: bfloat16 [8192, 4096], P('seq', 'tp')
Inputs may be any that keep to these rules, and one draw needn't show every extreme that they name: Each span number appears once; row r of hidden_in belongs to span span_order[r // 128].
All inputs are finite; a program needn't handle non-finite values.
Results may differ from a plain program's by a relative error of at most 0.014.
Values may be sent and summed in bfloat16 or wider, within the bound.
A program may use at most 64 MiB of HBM per device.

v0:
```python
import functools
import math

import jax
import jax.numpy as jnp
from jax import lax
from jax.experimental import pallas as pl
from jax.experimental.pallas import tpu as pltpu
from jax.sharding import Mesh
from jax.sharding import PartitionSpec as P

MODEL_WIDTH = 4096
HEAD_SIZE = 128
GROUP = 4
TOK = 128
NZ, NX, NC, NY = 8, 4, 2, 8
PLANE = NZ * NX
BLOCKS = PLANE * NC
COLS = MODEL_WIDTH // NY
WROWS = MODEL_WIDTH // BLOCKS
SUBS = 2
SEQ = ("z", "x", "c")
MESH_ID = pl.DeviceIdType.MESH

eps = 1e-06
rope_base = 1000000.0
exponent_scale = math.log2(math.e) / math.sqrt(HEAD_SIZE)


def x_first_tree():
    parent = {(1, 0): (0, 0), (-1, 0): (0, 0), (2, 0): (1, 0)}
    for dx in (0, 1, -1, 2):
        for dz in (1, 2, 3):
            parent[dx, dz] = (dx, dz - 1)
            parent[dx, -dz] = (dx, 1 - dz)
        parent[dx, 4] = (dx, 3) if dx in (0, 1) else (dx, -3)
    return parent


def z_first_tree():
    parent = {(0, 4): (0, 3)}
    for dz in (1, 2, 3):
        parent[0, dz] = (0, dz - 1)
        parent[0, -dz] = (0, 1 - dz)
    for dz in range(-3, 5):
        parent[1, dz] = (0, dz)
        parent[-1, dz] = (0, dz)
        parent[2, dz] = (1, dz) if dz % 2 == 0 else (-1, dz)
    return parent


def levels_of(parent):
    depth = {(0, 0): 0}

    def depth_of(o):
        if o not in depth:
            depth[o] = depth_of(parent[o]) + 1
        return depth[o]

    levels = [[] for _ in range(7)]
    for o in [(0, 0)] + list(parent):
        levels[depth_of(o)].append(o)
    return levels


def slot(o):
    return (o[1] % NZ) * NX + o[0] % NX


class Gather:
    def __init__(self, parent, buf, arrive, handed, sent, place, by_row):
        self.parent, self.buf, self.arrive = parent, buf, arrive
        self.handed, self.sent, self.place, self.by_row = handed, sent, place, by_row
        self.levels = levels_of(parent)

    def index(self, o):
        z, x, c, y = self.place
        return (lax.rem(z - o[1] + NZ, NZ) * NX + lax.rem(x - o[0] + NX, NX)) * NC + c

    def to(self, src, device, sem):
        return pltpu.make_async_remote_copy(
            src_ref=src,
            dst_ref=src,
            send_sem=self.sent.at[0],
            recv_sem=sem,
            device_id=device,
            device_id_type=MESH_ID,
        )

    def send(self, o):
        z, x, c, y = self.place
        block = self.buf.at[self.index(o)]
        for child, above in self.parent.items():
            if above == o:
                dx = (child[0] - o[0] + 1) % NX - 1
                dz = (child[1] - o[1] + 1) % NZ - 1
                near = (lax.rem(z + dz + NZ, NZ), lax.rem(x + dx + NX, NX), c, y)
                self.to(block, near, self.arrive.at[slot(child)]).start()
        row = o[1] % NZ if self.by_row else 0
        self.to(block, (z, x, 1 - c, y), self.handed.at[row]).start()

    def round(self, level):
        z, x, c, y = self.place
        for o in self.levels[level]:
            if level:
                block = self.buf.at[self.index(o)]
                self.to(block, (z, x, 1 - c, y), self.arrive.at[slot(o)]).wait_recv()
            self.send(o)

    def wait_handed(self, row=0):
        part = self.buf.at[pl.ds(0, NX if self.by_row else PLANE)]
        pltpu.make_async_copy(part, part, self.handed.at[row]).wait()

    def wait_sent(self):
        part = self.buf.at[pl.ds(0, BLOCKS - 1)]
        pltpu.make_async_copy(part, part, self.sent.at[0]).wait()


def kernel(
    hidden_ref,
    gain_ref,
    wq_ref,
    wkv_ref,
    wo_ref,
    bq_ref,
    bkv_ref,
    post_ref,
    rope_ref,
    qpos_ref,
    kpos_ref,
    attn_ref,
    normed_ref,
    hid,
    gains,
    wkv,
    wq,
    kv,
    wo,
    u,
    inv,
    qs,
    top,
    total,
    acc,
    attended,
    plus_in,
    minus_in,
    plus_out,
    minus_out,
    stats,
    local_sem,
    hid_arrive,
    hid_sent,
    gain_arrive,
    gain_sent,
    wkv_arrive,
    wkv_handed,
    wkv_sent,
    wq_arrive,
    wq_handed,
    wq_sent,
    kv_arrive,
    kv_handed,
    kv_sent,
    wo_arrive,
    wo_handed,
    wo_sent,
    plus_arrive,
    plus_sent,
    minus_arrive,
    minus_sent,
    stats_arrive,
    stats_sent,
):
    z, x, c, y = (lax.axis_index(n) for n in ("z", "x", "c", "y"))
    place = (z, x, c, y)
    me = (z * NX + x) * NC + c

    def y_near(d):
        return (z, x, c, lax.rem(y + d + NY, NY))

    def y_at(d):
        return lax.rem(y + d + NY, NY)

    starts = [
        pltpu.make_async_copy(wkv_ref, wkv.at[me], local_sem.at[0]),
        pltpu.make_async_copy(hidden_ref, hid.at[y], local_sem.at[1]),
        pltpu.make_async_copy(wq_ref, wq.at[me], local_sem.at[2]),
    ]
    for s in starts:
        s.start()
    gains[y] = jnp.broadcast_to(gain_ref[...].astype(jnp.float32), (8, COLS))
    barrier = pltpu.get_barrier_semaphore()
    friends = [(z, x, 1 - c, y)]
    friends += [(lax.rem(z + d, NZ), x, c, y) for d in (1, NZ - 1)]
    friends += [(z, lax.rem(x + d, NX), c, y) for d in (1, NX - 1)]
    friends += [(z, x, c, lax.rem(y + d, NY)) for d in range(1, NY)]
    for f in friends:
        pl.semaphore_signal(barrier, inc=1, device_id=f, device_id_type=MESH_ID)
    pl.semaphore_wait(barrier, len(friends))

    tree_a, tree_b = x_first_tree(), z_first_tree()
    g_wkv = Gather(tree_a, wkv, wkv_arrive, wkv_handed, wkv_sent, place, False)
    g_wq = Gather(tree_b, wq, wq_arrive, wq_handed, wq_sent, place, False)
    g_kv = Gather(tree_a, kv, kv_arrive, kv_handed, kv_sent, place, True)
    g_wo = Gather(tree_b, wo, wo_arrive, wo_handed, wo_sent, place, False)

    def remote(src, dst, sent, arrive, device):
        return pltpu.make_async_remote_copy(
            src_ref=src,
            dst_ref=dst,
            send_sem=sent,
            recv_sem=arrive,
            device_id=device,
            device_id_type=MESH_ID,
        )

    def hid_copy(step, sign):
        block = hid.at[y_at(-sign * step)]
        if step == 3:
            block = block.at[pl.ds(0 if sign > 0 else TOK // 2, TOK // 2)]
        k = step * 2 + (sign > 0)
        return remote(block, block, hid_sent.at[k], hid_arrive.at[k], y_near(sign))

    def hid_send(step):
        for sign in (1, -1):
            hid_copy(step, sign).start()

    def hid_wait(step):
        for sign in (1, -1):
            block = hid.at[y_at(-sign * (step + 1))]
            if step == 3:
                block = block.at[pl.ds(0 if sign > 0 else TOK // 2, TOK // 2)]
            k = step * 2 + (sign > 0)
            remote(block, block, hid_sent.at[k], hid_arrive.at[k], y_near(sign)).wait_recv()

    def gain_copy(d, source):
        block = gains.at[source]
        return remote(block, block, gain_sent.at[d], gain_arrive.at[d], y_near(d))

    starts[0].wait()
    g_wkv.round(0)
    starts[1].wait()
    hid_send(0)
    for d in range(1, NY):
        gain_copy(d, y).start()
    starts[2].wait()
    g_wq.round(0)

    wo[me] = wo_ref[...].astype(jnp.float32).T.astype(jnp.bfloat16)

    def prepare(source, d, first=False):
        if d:
            gain_copy(d % NY, source).wait_recv()
        h = hid[source].astype(jnp.float32)
        g = gains[source][0:1, :]
        u[source] = (h * g).astype(jnp.bfloat16)
        squares = h * h
        part = squares[:, 0:128]
        for k in range(1, COLS // 128):
            part = part + squares[:, k * 128 : (k + 1) * 128]
        inv[...] = part if first else inv[...] + part

    prepare(y, 0, True)
    for r in range(1, 5):
        g_wkv.round(r)
        hid_wait(r - 1)
        if r < 4:
            hid_send(r)
            prepare(y_at(r), -r)
            prepare(y_at(-r), r)
        else:
            prepare(y_at(4), 4)
        g_wq.round(r)
    g_wkv.round(5)
    g_wq.round(5)
    g_wkv.round(6)
    g_wkv.wait_handed()

    row_sum = jnp.sum(inv[...], axis=1, keepdims=True)
    row_scale = lax.rsqrt(row_sum / MODEL_WIDTH + eps)
    inv[...] = jnp.broadcast_to(row_scale, (TOK, 128))

    def project(weights, width):
        def step(k, total):
            block = weights[pl.ds(k * (BLOCKS // NY), BLOCKS // NY)].reshape(COLS, width)
            return total + jnp.dot(u[k], block, preferred_element_type=jnp.float32)

        return lax.fori_loop(0, NY, step, jnp.zeros((TOK, width), jnp.float32))

    def rotate(head):
        return head * rope_ref[0] + pltpu.roll(head, HEAD_SIZE // 2, 1) * rope_ref[1]

    pair = project(wkv, 2 * HEAD_SIZE)
    scale = inv[...]
    keys = pair[:, :HEAD_SIZE] * scale + bkv_ref[0:1, :].astype(jnp.float32)
    values = pair[:, HEAD_SIZE:] * scale + bkv_ref[1:2, :].astype(jnp.float32)
    kv[me, :, 0:HEAD_SIZE] = rotate(keys).astype(jnp.bfloat16)
    kv[me, :, HEAD_SIZE : 2 * HEAD_SIZE] = values.astype(jnp.bfloat16)
    g_wq.round(6)
    g_kv.round(0)
    g_wo.round(0)
    g_wq.wait_handed()

    query = project(wq, COLS)
    for g in range(GROUP):
        lanes = slice(g * HEAD_SIZE, (g + 1) * HEAD_SIZE)
        one = query[:, lanes] * inv[...] + bq_ref[0:1, lanes].astype(jnp.float32)
        qs[g] = rotate(one).astype(jnp.bfloat16)

    def attend(row, first):
        seq_row = lax.rem(z - row + NZ, NZ)
        chunk = NX * NC * TOK

        def head(g, carry):
            block = kv[pl.ds(seq_row * NX * NC, NX * NC)].reshape(chunk, 2 * HEAD_SIZE)
            scores = lax.dot_general(
                qs[g],
                block[:, :HEAD_SIZE],
                (((1,), (1,)), ((), ())),
                preferred_element_type=jnp.float32,
            )
            allowed = kpos_ref[pl.ds(seq_row, 1), :] <= qpos_ref[:, 0:1]
            scores = jnp.where(allowed, scores * exponent_scale, -1e30)
            peak = jnp.max(scores, axis=1, keepdims=True)
            if not first:
                old = top[g][:, 0:1]
                peak = jnp.maximum(old, peak)
            weights = jnp.exp2(scores - peak)
            count = jnp.sum(weights, axis=1, keepdims=True)
            summed = jnp.dot(
                weights.astype(jnp.bfloat16),
                block[:, HEAD_SIZE:],
                preferred_element_type=jnp.float32,
            )
            if not first:
                factor = jnp.exp2(old - peak)
                count = count + total[g][:, 0:1] * factor
                summed = summed + acc[g] * factor
            top[g] = jnp.broadcast_to(peak, (TOK, 128))
            total[g] = jnp.broadcast_to(count, (TOK, 128))
            acc[g] = summed
            return carry

        lax.fori_loop(0, GROUP, head, 0)

    for r in range(1, 7):
        g_kv.round(r)
        g_wo.round(r)
        if r >= 2:
            for row in sorted({r - 2, 2 - r} if r < 6 else {4}):
                g_kv.wait_handed(row % NZ)
                attend(row, r == 2)
    for g in range(GROUP):
        attended[:, g * HEAD_SIZE : (g + 1) * HEAD_SIZE] = (acc[g] / total[g]).astype(jnp.bfloat16)
    g_wo.wait_handed()

    def partial(target):
        block = wo[pl.ds(target * (BLOCKS // NY), BLOCKS // NY)].reshape(COLS, COLS)
        return lax.dot_general(
            attended[...], block, (((1,), (1,)), ((), ())), preferred_element_type=jnp.float32
        )

    sub = TOK // SUBS
    half = COLS // 2

    def sum_copy(step, sign, piece):
        outs, ins, sent, arrive = (
            (plus_out, plus_in, plus_sent, plus_arrive)
            if sign > 0
            else (minus_out, minus_in, minus_sent, minus_arrive)
        )
        rows = pl.ds(piece * sub, sub)
        lanes = pl.ds(0, COLS)
        if step == 0:
            lanes = pl.ds(0 if sign > 0 else half, half)
        k = step * SUBS + piece
        return remote(
            outs.at[step, rows, lanes],
            ins.at[step, rows, lanes],
            sent.at[k],
            arrive.at[k],
            y_near(sign),
        )

    far = partial(y_at(4)).astype(jnp.bfloat16)
    plus_out[0, :, 0:half] = far[:, :half]
    minus_out[0, :, half:COLS] = far[:, half:]
    for piece in range(SUBS):
        sum_copy(0, 1, piece).start()
        sum_copy(0, -1, piece).start()
    for step in range(1, 4):
        terms = {1: partial(y_at(4 - step)), -1: partial(y_at(step - 4))}
        for piece in range(SUBS):
            rows = slice(piece * sub, (piece + 1) * sub)
            for sign in (1, -1):
                outs, ins = (plus_out, plus_in) if sign > 0 else (minus_out, minus_in)
                sum_copy(step - 1, sign, piece).wait_recv()
                term = terms[sign][rows]
                if step == 1:
                    lanes = slice(0, half) if sign > 0 else slice(half, COLS)
                    other = slice(half, COLS) if sign > 0 else slice(0, half)
                    got = ins[0, rows, lanes].astype(jnp.float32)
                    outs[1, rows, lanes] = (term[:, lanes] + got).astype(jnp.bfloat16)
                    outs[1, rows, other] = term[:, other].astype(jnp.bfloat16)
                else:
                    got = ins[step - 1, rows].astype(jnp.float32)
                    outs[step, rows] = (term + got).astype(jnp.bfloat16)
                sum_copy(step, sign, piece).start()
    own = partial(y)
    for piece in range(SUBS):
        rows = slice(piece * sub, (piece + 1) * sub)
        for sign in (1, -1):
            sum_copy(3, sign, piece).wait_recv()
        mixed = (
            own[rows]
            + plus_in[3, rows].astype(jnp.float32)
            + minus_in[3, rows].astype(jnp.float32)
        )
        attn_ref[rows, :] = mixed.astype(jnp.bfloat16)
        stream = hid[y, rows].astype(jnp.float32) + mixed
        squares = stream * stream
        part = squares[:, 0:128]
        for k in range(1, COLS // 128):
            part = part + squares[:, k * 128 : (k + 1) * 128]
        inv[rows, :] = part
        for g in range(GROUP):
            acc[g, rows, :] = stream[:, g * 128 : (g + 1) * 128]

    column = jnp.sum(inv[...], axis=1, keepdims=True)
    stats[y] = jnp.broadcast_to(column, (TOK, 128)).T[0:8, :]

    def stats_copy(d, source):
        block = stats.at[source]
        return remote(block, block, stats_sent.at[d], stats_arrive.at[d], y_near(d))

    for d in range(1, NY):
        stats_copy(d, y).start()
    for g in (g_wkv, g_wq, g_kv, g_wo):
        g.wait_sent()
    for step in range(4):
        for sign in (1, -1):
            hid_copy(step, sign).wait_send()
            for piece in range(SUBS):
                sum_copy(step, sign, piece).wait_send()
    for d in range(1, NY):
        gain_copy(d, y).wait_send()
    for d in range(1, NY):
        stats_copy(d, y_at(-d)).wait_recv()
    summed = stats[0]
    for k in range(1, NY):
        summed = summed + stats[k]
    rows = jnp.broadcast_to(summed[0:1, :], (128, TOK)).T
    scale = lax.rsqrt(rows / MODEL_WIDTH + eps)
    for g in range(GROUP):
        lanes = slice(g * 128, (g + 1) * 128)
        gain = post_ref[0:1, lanes].astype(jnp.float32)
        normed_ref[:, lanes] = (acc[g] * scale * gain).astype(jnp.bfloat16)
    for d in range(1, NY):
        stats_copy(d, y).wait_send()


def per_device(
    hidden_in,
    span_order,
    norm_gain,
    w_query,
    bias_query,
    key_value_weight,
    bias_kv,
    w_out,
    post_gain,
):
    seq_index = lax.axis_index(SEQ)
    own_span = jnp.sum(jnp.where(jnp.arange(BLOCKS) == seq_index, span_order, 0))
    inside = jnp.arange(TOK, dtype=jnp.int32)
    positions = own_span * TOK + inside
    key_positions = (span_order[:, None] * TOK + inside[None, :]).reshape(NZ, NX * NC * TOK)
    lane = jnp.arange(HEAD_SIZE, dtype=jnp.int32)
    pair = (lane % (HEAD_SIZE // 2)).astype(jnp.float32)
    inverse = jnp.exp(-math.log(rope_base) * pair / (HEAD_SIZE // 2))
    angles = positions.astype(jnp.float32)[:, None] * inverse[None, :]
    sign = jnp.where(lane < HEAD_SIZE // 2, -1.0, 1.0)
    rope = jnp.stack([jnp.cos(angles), jnp.sin(angles) * sign[None, :]])
    query_positions = jnp.broadcast_to(positions[:, None], (TOK, 128))

    bf16, f32 = jnp.bfloat16, jnp.float32
    vmem = pl.BlockSpec(memory_space=pltpu.VMEM)
    anywhere = pl.BlockSpec(memory_space=pl.ANY)
    dma = pltpu.SemaphoreType.DMA
    out = jax.ShapeDtypeStruct((TOK, COLS), bf16)
    gathers = []
    for rows in (1, 1, NZ, 1):
        gathers += [dma((PLANE,)), dma((rows,)), dma((1,))]
    return pl.pallas_call(
        kernel,
        out_shape=(out, out),
        in_specs=[anywhere, vmem, anywhere, anywhere] + [vmem] * 7,
        out_specs=(vmem, vmem),
        scratch_shapes=[
            pltpu.VMEM((NY, TOK, COLS), bf16),
            pltpu.VMEM((NY, 8, COLS), f32),
            pltpu.VMEM((BLOCKS, WROWS, 2 * HEAD_SIZE), bf16),
            pltpu.VMEM((BLOCKS, WROWS, COLS), bf16),
            pltpu.VMEM((BLOCKS, TOK, 2 * HEAD_SIZE), bf16),
            pltpu.VMEM((BLOCKS, WROWS, COLS), bf16),
            pltpu.VMEM((NY, TOK, COLS), bf16),
            pltpu.VMEM((TOK, 128), f32),
            pltpu.VMEM((GROUP, TOK, HEAD_SIZE), bf16),
            pltpu.VMEM((GROUP, TOK, 128), f32),
            pltpu.VMEM((GROUP, TOK, 128), f32),
            pltpu.VMEM((GROUP, TOK, 128), f32),
            pltpu.VMEM((TOK, COLS), bf16),
            pltpu.VMEM((4, TOK, COLS), bf16),
            pltpu.VMEM((4, TOK, COLS), bf16),
            pltpu.VMEM((4, TOK, COLS), bf16),
            pltpu.VMEM((4, TOK, COLS), bf16),
            pltpu.VMEM((NY, 8, 128), f32),
            dma((3,)),
            dma((8,)),
            dma((8,)),
            dma((NY,)),
            dma((NY,)),
            *gathers,
            dma((4 * SUBS,)),
            dma((4 * SUBS,)),
            dma((4 * SUBS,)),
            dma((4 * SUBS,)),
            dma((NY,)),
            dma((NY,)),
        ],
        compiler_params=pltpu.CompilerParams(
            collective_id=0, has_side_effects=True, vmem_limit_bytes=56 << 20
        ),
    )(
        hidden_in,
        norm_gain.reshape(1, COLS),
        w_query,
        key_value_weight.reshape(WROWS, 2 * HEAD_SIZE),
        w_out,
        bias_query.reshape(1, COLS),
        bias_kv,
        post_gain.reshape(1, COLS),
        rope,
        query_positions,
        key_positions,
    )


def solution(mesh):
    torus = Mesh(mesh.devices.reshape(NZ, NX, NC, NY), ("z", "x", "c", "y"))
    in_specs = (
        P(SEQ, "y"),
        P(),
        P("y"),
        P(SEQ, "y"),
        P("y"),
        P(SEQ, None, "y"),
        P(None, "y"),
        P("y", SEQ),
        P("y"),
    )
    out_specs = (P(SEQ, "y"), P(SEQ, "y"))
    return jax.shard_map(
        per_device, mesh=torus, in_specs=in_specs, out_specs=out_specs, check_vma=False
    )
```

profile of v0, /device:TPU:2, one launch (start us, length us, event | category | flops | bytes accessed | tf_op | source)
XLA Modules:
  0.0 122.5 jit_solution(17103183434979045252)
XLA Ops:
  0.6 0.0 copy-start.6
  0.6 0.6 copy-done.6
  1.3 0.6 broadcast_multiply_fusion
  2.6 0.0 copy-start.3
  2.6 0.7 copy-done.3
  3.3 0.0 copy-start.4
  3.3 0.0 copy-start.5
  3.3 0.6 reshape.160.gain_ref
  3.9 0.1 copy-done.4
  4.0 0.0 copy-start.2
  4.0 0.6 reshape.162.bq_ref
  4.5 0.0 copy-done.5
  4.5 0.6 reshape.163.post_ref
  5.1 0.1 add.56
  5.2 0.1 copy.11
  5.3 0.7 bitcast_add_fusion.kpos_ref
  6.0 0.0 copy-done.2
  6.0 0.6 copy.15
  6.6 0.7 broadcast_in_dim.26.qpos_ref
  7.3 0.3 multiply_cosine_fusion
  7.6 0.0 copy-start.1
  7.6 0.7 pad_maximum_fusion.rope_ref
  8.3 0.2 copy-done.1
  8.4 0.8 copy.12.wo_ref
  9.2 111.0 %shard_map.104 = (bf16[128,512]{1,0:T(8,128)(2,1)}, bf16[128,512]{1,0:T(8,128)(2,1)}) custom-call(bf16[128,512]{1,0:T(8,128)(2,1)} %hidden_ref.1, bf16[1,512]{1,0:T(2,128)(2,1)} %reshape.160.gain_ref, bf16[64,512]{1,0:T(8,128)(2,1)} %wq_ref.1, bf16[64,256]{1,0:T(8,128)(2,1)} %bitcast.8, bf16[512,64]{1,0:T(8,128)(2,1)} %copy.12.wo_ref, ...), custom_call_target="tpu_custom_call" | custom-call | tf_op jit(solution)/shard_map/pallas_call | solution.py:495
  120.2 0.0 copy-start
  120.2 1.6 %copy.18 = bf16[128,512]{1,0:T(8,128)(2,1)} copy(bf16[128,512]{1,0:T(8,128)(2,1)} %get-tuple-element.12) | data formatting | bytes 262144
  121.8 0.0 copy-done
  121.8 0.7 copy.19
  (3 shorter events, 0.0 us)
Async XLA Ops:
  0.6 0.7 copy-start.6
  2.6 0.7 copy-start.3
  3.3 0.7 copy-start.4
  3.3 1.3 %copy-start.5 = (bf16[512]{0:T(512)(128)(2,1)S(1)}, bf16[512]{0:T(512)(128)(2,1)}, u32[]{:S(2)}) copy-start(bf16[512]{0:T(512)(128)(2,1)} %param.17) | copy-start | bytes 3076
  4.0 2.0 %copy-start.2 = (bf16[64,2,128]{2,1,0:T(2,128)(2,1)S(1)}, bf16[64,2,128]{2,1,0:T(2,128)(2,1)}, u32[]{:S(2)}) copy-start(bf16[64,2,128]{2,1,0:T(2,128)(2,1)} %param.14) | copy-start | bytes 98308
  7.6 0.8 copy-start.1
  120.2 1.6 %copy-start = (bf16[128,512]{1,0:T(8,128)(2,1)S(1)}, bf16[128,512]{1,0:T(8,128)(2,1)}, u32[]{:S(2)}) copy-start(bf16[128,512]{1,0:T(8,128)(2,1)} %get-tuple-element.13) | copy-start | bytes 393220
where the time goes:
time: 123 us; the launch traced here: 122 us
  Pallas kernels  111 us (90%)
  local copies, waits for them, and re-layouts  7.83 us (6%)
  other arithmetic  2.3 us (2%)
  between operations  1.36 us (1%)
    pallas_call x1, Pallas kernels, per_device(): pl.pallas_call(kernel, out_shape=(out, out), in_specs=[anywhere, vmem, an...  111 us
    unnamed x18, local copies, waits for them, and re-layouts  5.22 us

commit v1 on v0

v1 whole, which is shorter than its diff:
```python
import heapq
import math

import jax
import jax.numpy as jnp
import numpy as np
from jax import lax
from jax.experimental import pallas as pl
from jax.experimental.pallas import tpu as pltpu
from jax.sharding import Mesh
from jax.sharding import PartitionSpec as P

MODEL_WIDTH = 4096
HEAD_SIZE = 128
GROUP = 4
TOK = 128
NZ, NX, NC, NY = 8, 4, 2, 8
PLANE = NZ * NX
BLOCKS = PLANE * NC
COLS = MODEL_WIDTH // NY
WROWS = MODEL_WIDTH // BLOCKS
SUBS = 4
HALVES = 2
SEQ = ("z", "x", "c")
MESH_ID = pl.DeviceIdType.MESH

eps = 1e-06
rope_base = 1000000.0
exponent_scale = math.log2(math.e) / math.sqrt(HEAD_SIZE)

RATE, HOP, FURTHER, HOP_Y, HAND = 46.6, 3.3, 0.7, 2.1, 1.6
WO_START = 12.0


def x_then_z(direct_x):
    parent = {(2, 0): (0, 0) if direct_x else (1, 0), (1, 0): (0, 0), (-1, 0): (0, 0)}
    for dx in (0, 1, -1, 2):
        for dz in (1, 2, 3):
            parent[dx, dz] = (dx, dz - 1)
            parent[dx, -dz] = (dx, 1 - dz)
        parent[dx, 4] = (dx, 3) if dx in (0, 1) else (dx, -3)
    return parent


def z_then_x(reach):
    parent = {}
    for far in (4, 3, -3, 2, -2, 1, -1):
        step = (abs(far) - 1) // reach * reach
        parent[0, far] = (0, step if far > 0 else -step)
    for dz in range(-3, 5):
        parent[1, dz] = (0, dz)
        parent[-1, dz] = (0, dz)
        parent[2, dz] = (1, dz) if dz % 2 == 0 else (-1, dz)
    return parent


TREES = {
    "wkv": z_then_x(4),
    "wq": x_then_z(True),
    "wo": z_then_x(1),
    "k": z_then_x(2),
    "v": x_then_z(False),
}
KB = {"wkv": 32, "wq": 64, "wo": 64, "k": 32, "v": 32}


def away(child, parent):
    dx = (child[0] - parent[0] + 1) % NX - 1
    dz = (child[1] - parent[1] + 3) % NZ - 3
    return dx, dz


def children_of(tree):
    below = {}
    for child, parent in tree.items():
        below.setdefault(parent, []).append(child)
    return below


def planned_steps():
    below = {g: children_of(t) for g, t in TREES.items()}
    free, heap, steps = {}, [], []
    got, tail = dict.fromkeys(TREES, 0), dict.fromkeys(TREES, 0.0)
    rows_in, waiting = {}, []
    now, hidden_left = 0.0, 6 * HALVES + 2
    keys_done = query_done = own_row_done = False

    def push(t, *what):
        heapq.heappush(heap, (round(t, 6), len(steps), len(heap), what))

    def transfer(route, kb, latency):
        end, hops = now, 0
        for link, n in route:
            free[link] = max(free.get(link, 0.0), now) + kb * n / RATE
            end, hops = max(end, free[link]), hops + n
        return end + latency + FURTHER * (hops - 1)

    push(0.0, "wkv", (0, 0))
    push(0.0, "wq", (0, 0))
    push(WO_START, "wo", (0, 0))
    for piece in range(HALVES):
        for sign in (1, -1):
            push(0.05, "hid", 0, sign, piece)
    while True:
        ahead = heap[0][0] if heap else math.inf
        keys_at = max(now, tail["wkv"] + HAND)
        query_at = max(now, tail["wq"] + HAND)
        if not keys_done and got["wkv"] == PLANE and not hidden_left and ahead >= keys_at - 0.3:
            now, keys_done = keys_at + 1.8, True
            steps.append(("keys",))
            push(now, "k", (0, 0))
            push(now + 0.01, "v", (0, 0))
            continue
        if keys_done and not query_done and got["wq"] == PLANE and ahead >= query_at - 0.3:
            now, query_done = query_at + 2.5, True
            steps.append(("query",))
            continue
        able = [w for w in waiting if own_row_done or w[1] == 0]
        if query_done and able and ahead >= max(now, able[0][0]) - 0.2:
            waiting.remove(able[0])
            now = max(now, able[0][0]) + 0.9
            own_row_done = True
            steps.append(("attend", able[0][1]))
            continue
        if not heap:
            return steps
        at, _, _, what = heapq.heappop(heap)
        now = max(now, at) + 0.03
        steps.append(what)
        if what[0] == "hid":
            _, hop, sign, piece = what
            if hop:
                hidden_left -= 1
                now += 0.25 / HALVES
            if hop < 3 or (hop == 3 and piece == (sign < 0)):
                route = [("y+" if sign > 0 else "y-", 1)]
                kb = TOK / HALVES
                push(transfer(route, kb, HOP_Y), "hid", hop + 1, sign, piece)
            continue
        g, o = what
        got[g] += 1
        tail[g] = max(tail[g], now)
        for child in below[g].get(o, ()):
            dx, dz = away(child, o)
            route = [("x+" if dx > 0 else "x-", abs(dx))] if dx else []
            route += [("z+" if dz > 0 else "z-", abs(dz))] if dz else []
            now += 0.03
            push(transfer(route, KB[g], HOP), g, child)
        now += 0.03
        if g in ("k", "v"):
            rows_in[o[1]] = rows_in.get(o[1], 0) + 1
            if rows_in[o[1]] == 2 * NX:
                waiting.append((now + HAND, o[1]))


class Gather:
    def __init__(self, tree, buf, arrive, handed, sent, place, by_row):
        self.below, self.buf, self.arrive = children_of(tree), buf, arrive
        self.handed, self.sent, self.place, self.by_row = handed, sent, place, by_row

    def index(self, o):
        z, x, c, y = self.place
        return (lax.rem(z - o[1] + NZ, NZ) * NX + lax.rem(x - o[0] + NX, NX)) * NC + c

    def slot(self, o):
        return (o[1] % NZ) * NX + o[0] % NX

    def to(self, src, device, sem):
        return pltpu.make_async_remote_copy(
            src_ref=src,
            dst_ref=src,
            send_sem=self.sent.at[0],
            recv_sem=sem,
            device_id=device,
            device_id_type=MESH_ID,
        )

    def arrived(self, o):
        z, x, c, y = self.place
        block = self.buf.at[self.index(o)]
        partner = (z, x, 1 - c, y)
        if o != (0, 0):
            self.to(block, partner, self.arrive.at[self.slot(o)]).wait_recv()
        for child in self.below.get(o, ()):
            dx, dz = away(child, o)
            near = (lax.rem(z + dz + NZ, NZ), lax.rem(x + dx + NX, NX), c, y)
            self.to(block, near, self.arrive.at[self.slot(child)]).start()
        row = o[1] % NZ if self.by_row else 0
        self.to(block, partner, self.handed.at[row]).start()

    def wait_handed(self, row=0):
        part = self.buf.at[pl.ds(0, NX if self.by_row else PLANE)]
        pltpu.make_async_copy(part, part, self.handed.at[row]).wait()

    def wait_sent(self):
        part = self.buf.at[pl.ds(0, BLOCKS - 1)]
        pltpu.make_async_copy(part, part, self.sent.at[0]).wait()


def kernel(
    hidden_ref,
    wq_ref,
    wkv_ref,
    wo_ref,
    span_ref,
    gain_ref,
    bq_ref,
    bkv_ref,
    inside_ref,
    spans_ref,
    mixed_ref,
    scale_ref,
    hid,
    gains,
    wkv,
    wq,
    wo,
    ks,
    vs,
    u,
    inv,
    rope,
    kpos,
    qs,
    top,
    total,
    acc,
    attended,
    plus_in,
    minus_in,
    plus_out,
    minus_out,
    stats,
    local_sem,
    hid_arrive,
    hid_sent,
    gain_arrive,
    gain_sent,
    wkv_arrive,
    wkv_handed,
    wkv_sent,
    wq_arrive,
    wq_handed,
    wq_sent,
    wo_arrive,
    wo_handed,
    wo_sent,
    k_arrive,
    k_handed,
    k_sent,
    v_arrive,
    v_handed,
    v_sent,
    plus_arrive,
    plus_sent,
    minus_arrive,
    minus_sent,
    stats_arrive,
    stats_sent,
):
    z, x, c, y = (lax.axis_index(n) for n in ("z", "x", "c", "y"))
    place = (z, x, c, y)
    me = (z * NX + x) * NC + c

    def y_near(d):
        return (z, x, c, lax.rem(y + d + NY, NY))

    def y_at(d):
        return lax.rem(y + d + NY, NY)

    barrier = pltpu.get_barrier_semaphore()
    friends = [(z, x, 1 - c, y)]
    friends += [(lax.rem(z + d, NZ), x, c, y) for d in range(1, NZ)]
    friends += [(z, lax.rem(x + d, NX), c, y) for d in range(1, NX)]
    friends += [(z, x, c, lax.rem(y + d, NY)) for d in range(1, NY)]
    for f in friends:
        pl.semaphore_signal(barrier, inc=1, device_id=f, device_id_type=MESH_ID)
    starts = {
        "wkv": pltpu.make_async_copy(wkv_ref, wkv.at[me], local_sem.at[0]),
        "hid": pltpu.make_async_copy(hidden_ref, hid.at[y], local_sem.at[1]),
        "wq": pltpu.make_async_copy(wq_ref, wq.at[me], local_sem.at[2]),
        "wo": pltpu.make_async_copy(wo_ref, wo.at[me], local_sem.at[3]),
    }
    for s in starts.values():
        s.start()

    own_gain = gain_ref[...].astype(jnp.float32).reshape(1, COLS)
    gains[y] = jnp.broadcast_to(own_gain, (8, COLS))
    own_span = span_ref[me]
    of_span = spans_ref[own_span]
    cos_s, sin_s = of_span[0:1, :], of_span[1:2, :]
    rope[0] = inside_ref[0] * cos_s - inside_ref[1] * sin_s
    lanes = lax.broadcasted_iota(jnp.int32, (TOK, 128), 1)
    sine = inside_ref[1] * cos_s + inside_ref[0] * sin_s
    rope[1] = jnp.where(lanes < HEAD_SIZE // 2, -sine, sine)
    token = lax.broadcasted_iota(jnp.int32, (1, TOK), 1)
    for row in range(NZ):
        for k in range(NX * NC):
            where = slice(k * TOK, (k + 1) * TOK)
            kpos[row : row + 1, where] = token + span_ref[row * NX * NC + k] * TOK
    inv[...] = jnp.zeros_like(inv)
    pl.semaphore_wait(barrier, len(friends))

    gathers = {
        "wkv": Gather(TREES["wkv"], wkv, wkv_arrive, wkv_handed, wkv_sent, place, False),
        "wq": Gather(TREES["wq"], wq, wq_arrive, wq_handed, wq_sent, place, False),
        "wo": Gather(TREES["wo"], wo, wo_arrive, wo_handed, wo_sent, place, False),
        "k": Gather(TREES["k"], ks, k_arrive, k_handed, k_sent, place, True),
        "v": Gather(TREES["v"], vs, v_arrive, v_handed, v_sent, place, True),
    }

    def remote(src, dst, sent, arrive, device):
        return pltpu.make_async_remote_copy(
            src_ref=src,
            dst_ref=dst,
            send_sem=sent,
            recv_sem=arrive,
            device_id=device,
            device_id_type=MESH_ID,
        )

    part_rows = TOK // HALVES

    def hid_copy(hop, sign, piece, arriving=False):
        source = y_at(-sign * (hop + 1 if arriving else hop))
        block = hid.at[source, pl.ds(piece * part_rows, part_rows)]
        k = (hop * HALVES + piece) * 2 + (sign > 0)
        return remote(block, block, hid_sent.at[k], hid_arrive.at[k], y_near(sign))

    def hid_goes(hop, sign, piece):
        return hop < 3 or (hop == 3 and piece == (sign < 0))

    def gain_copy(d, source):
        block = gains.at[source]
        return remote(block, block, gain_sent.at[d], gain_arrive.at[d], y_near(d))

    def prepare(source, piece):
        rows = slice(piece * part_rows, (piece + 1) * part_rows)
        h = hid[source, rows].astype(jnp.float32)
        u[source, rows] = (h * gains[source][0:1, :]).astype(jnp.bfloat16)
        squares = h * h
        part = squares[:, 0:128]
        for k in range(1, COLS // 128):
            part = part + squares[:, k * 128 : (k + 1) * 128]
        inv[rows] = inv[rows] + part

    def project(weights, width):
        def step(k, total):
            block = weights[pl.ds(k * (BLOCKS // NY), BLOCKS // NY)].reshape(COLS, width)
            return total + jnp.dot(u[k], block, preferred_element_type=jnp.float32)

        return lax.fori_loop(0, NY, step, jnp.zeros((TOK, width), jnp.float32))

    def rotate(head):
        return head * rope[0] + pltpu.roll(head, HEAD_SIZE // 2, 1) * rope[1]

    def make_keys():
        row_sum = jnp.sum(inv[...], axis=1, keepdims=True)
        inv[...] = jnp.broadcast_to(lax.rsqrt(row_sum / MODEL_WIDTH + eps), (TOK, 128))
        pair = project(wkv, 2 * HEAD_SIZE)
        scale = inv[...]
        keys = pair[:, :HEAD_SIZE] * scale + bkv_ref[0:1, :].astype(jnp.float32)
        values = pair[:, HEAD_SIZE:] * scale + bkv_ref[1:2, :].astype(jnp.float32)
        ks[me] = rotate(keys).astype(jnp.bfloat16)
        vs[me] = values.astype(jnp.bfloat16)

    def make_query():
        query = project(wq, COLS)
        bias = bq_ref[...].astype(jnp.float32).reshape(1, COLS)
        for g in range(GROUP):
            lanes = slice(g * HEAD_SIZE, (g + 1) * HEAD_SIZE)
            qs[g] = rotate(query[:, lanes] * inv[...] + bias[:, lanes]).astype(jnp.bfloat16)

    def attend(row):
        first = row == 0
        seq_row = lax.rem(z - row + NZ, NZ)
        chunk = NX * NC * TOK
        query_pos = lax.broadcasted_iota(jnp.int32, (TOK, 128), 0) + own_span * TOK

        def head(g, carry):
            scores = lax.dot_general(
                qs[g],
                ks[pl.ds(seq_row * NX * NC, NX * NC)].reshape(chunk, HEAD_SIZE),
                (((1,), (1,)), ((), ())),
                preferred_element_type=jnp.float32,
            )
            allowed = kpos[pl.ds(seq_row, 1), :] <= query_pos[:, 0:1]
            scores = jnp.where(allowed, scores * exponent_scale, -1e30)
            peak = jnp.max(scores, axis=1, keepdims=True)
            if not first:
                old = top[g][:, 0:1]
                peak = jnp.maximum(old, peak)
            weights = jnp.exp2(scores - peak)
            count = jnp.sum(weights, axis=1, keepdims=True)
            summed = jnp.dot(
                weights.astype(jnp.bfloat16),
                vs[pl.ds(seq_row * NX * NC, NX * NC)].reshape(chunk, HEAD_SIZE),
                preferred_element_type=jnp.float32,
            )
            if not first:
                factor = jnp.exp2(old - peak)
                count = count + total[g][:, 0:1] * factor
                summed = summed + acc[g] * factor
            top[g] = jnp.broadcast_to(peak, (TOK, 128))
            total[g] = jnp.broadcast_to(count, (TOK, 128))
            acc[g] = summed
            return carry

        lax.fori_loop(0, GROUP, head, 0)

    seen_gain = {0}
    for step in planned_steps():
        if step[0] == "hid":
            _, hop, sign, piece = step
            if hop == 0:
                if piece == 0 and sign > 0:
                    starts["hid"].wait()
                hid_copy(0, sign, piece).start()
                if piece == HALVES - 1 and sign < 0:
                    for d in range(1, NY):
                        gain_copy(d, y).start()
                    for k in range(HALVES):
                        prepare(y, k)
            else:
                hid_copy(hop - 1, sign, piece, True).wait_recv()
                if hid_goes(hop, sign, piece):
                    hid_copy(hop, sign, piece).start()
                d = sign * hop % NY
                if d not in seen_gain:
                    seen_gain.add(d)
                    gain_copy(d, y_at(-d)).wait_recv()
                prepare(y_at(-d), piece)
        elif step[0] == "keys":
            gathers["wkv"].wait_handed()
            make_keys()
        elif step[0] == "query":
            gathers["wq"].wait_handed()
            make_query()
        elif step[0] == "attend":
            gathers["k"].wait_handed(step[1] % NZ)
            gathers["v"].wait_handed(step[1] % NZ)
            attend(step[1])
        else:
            g, o = step
            if o == (0, 0) and g in starts:
                starts[g].wait()
            gathers[g].arrived(o)
    for g in range(GROUP):
        attended[:, g * HEAD_SIZE : (g + 1) * HEAD_SIZE] = (acc[g] / total[g]).astype(jnp.bfloat16)
    gathers["wo"].wait_handed()

    def partial(target):
        block = wo[pl.ds(target * (BLOCKS // NY), BLOCKS // NY)].reshape(COLS, COLS)
        return lax.dot_general(
            attended[...], block, (((1,), (1,)), ((), ())), preferred_element_type=jnp.float32
        )

    sub = TOK // SUBS
    half = COLS // 2

    def sum_copy(step, sign, piece):
        outs, ins, sent, arrive = (
            (plus_out, plus_in, plus_sent, plus_arrive)
            if sign > 0
            else (minus_out, minus_in, minus_sent, minus_arrive)
        )
        rows = pl.ds(piece * sub, sub)
        lanes = pl.ds(0, COLS)
        if step == 0:
            lanes = pl.ds(0 if sign > 0 else half, half)
        k = step * SUBS + piece
        return remote(
            outs.at[step, rows, lanes],
            ins.at[step, rows, lanes],
            sent.at[k],
            arrive.at[k],
            y_near(sign),
        )

    far = partial(y_at(4)).astype(jnp.bfloat16)
    plus_out[0, :, 0:half] = far[:, :half]
    minus_out[0, :, half:COLS] = far[:, half:]
    for piece in range(SUBS):
        sum_copy(0, 1, piece).start()
        sum_copy(0, -1, piece).start()
    for step in range(1, 4):
        terms = {1: partial(y_at(4 - step)), -1: partial(y_at(step - 4))}
        for piece in range(SUBS):
            rows = slice(piece * sub, (piece + 1) * sub)
            for sign in (1, -1):
                outs, ins = (plus_out, plus_in) if sign > 0 else (minus_out, minus_in)
                sum_copy(step - 1, sign, piece).wait_recv()
                term = terms[sign][rows]
                if step == 1:
                    lanes = slice(0, half) if sign > 0 else slice(half, COLS)
                    other = slice(half, COLS) if sign > 0 else slice(0, half)
                    got = ins[0, rows, lanes].astype(jnp.float32)
                    outs[1, rows, lanes] = (term[:, lanes] + got).astype(jnp.bfloat16)
                    outs[1, rows, other] = term[:, other].astype(jnp.bfloat16)
                else:
                    got = ins[step - 1, rows].astype(jnp.float32)
                    outs[step, rows] = (term + got).astype(jnp.bfloat16)
                sum_copy(step, sign, piece).start()
    own = partial(y)
    for piece in range(SUBS):
        rows = slice(piece * sub, (piece + 1) * sub)
        for sign in (1, -1):
            sum_copy(3, sign, piece).wait_recv()
        mixed = (
            own[rows]
            + plus_in[3, rows].astype(jnp.float32)
            + minus_in[3, rows].astype(jnp.float32)
        )
        mixed_ref[rows, :] = mixed
        stream = hid[y, rows].astype(jnp.float32) + mixed
        squares = stream * stream
        part = squares[:, 0:128]
        for k in range(1, COLS // 128):
            part = part + squares[:, k * 128 : (k + 1) * 128]
        inv[rows, :] = part

    column = jnp.sum(inv[...], axis=1, keepdims=True)
    stats[y] = jnp.broadcast_to(column, (TOK, 128)).T[0:8, :]

    def stats_copy(d, source):
        block = stats.at[source]
        return remote(block, block, stats_sent.at[d], stats_arrive.at[d], y_near(d))

    for d in range(1, NY):
        stats_copy(d, y).start()
    for g in gathers.values():
        g.wait_sent()
    for step in range(4):
        for sign in (1, -1):
            for piece in range(HALVES):
                if hid_goes(step, sign, piece):
                    hid_copy(step, sign, piece).wait_send()
            for piece in range(SUBS):
                sum_copy(step, sign, piece).wait_send()
    for d in range(1, NY):
        gain_copy(d, y).wait_send()
    for d in range(1, NY):
        stats_copy(d, y_at(-d)).wait_recv()
    summed = stats[0]
    for k in range(1, NY):
        summed = summed + stats[k]
    rows = jnp.broadcast_to(summed[0:1, :], (128, TOK)).T
    scale_ref[...] = lax.rsqrt(rows / MODEL_WIDTH + eps)
    for d in range(1, NY):
        stats_copy(d, y).wait_send()


def per_device(
    hidden_in,
    span_order,
    norm_gain,
    w_query,
    bias_query,
    key_value_weight,
    bias_kv,
    w_out,
    post_gain,
):
    half = HEAD_SIZE // 2
    inverse = rope_base ** (-(np.arange(HEAD_SIZE) % half) / half)
    row_angles = np.arange(TOK)[:, None] * inverse[None, :]
    span_angles = np.arange(BLOCKS)[:, None] * TOK * inverse[None, :]
    inside = np.stack([np.cos(row_angles), np.sin(row_angles)]).astype(np.float32)
    spans = np.stack([np.cos(span_angles), np.sin(span_angles)], axis=1).astype(np.float32)

    bf16, f32 = jnp.bfloat16, jnp.float32
    vmem = pl.BlockSpec(memory_space=pltpu.VMEM)
    smem = pl.BlockSpec(memory_space=pltpu.SMEM)
    anywhere = pl.BlockSpec(memory_space=pl.ANY)
    dma = pltpu.SemaphoreType.DMA
    gathers = []
    for rows in (1, 1, 1, NZ, NZ):
        gathers += [dma((PLANE,)), dma((rows,)), dma((1,))]
    mixed, scale = pl.pallas_call(
        kernel,
        out_shape=(
            jax.ShapeDtypeStruct((TOK, COLS), f32),
            jax.ShapeDtypeStruct((TOK, 128), f32),
        ),
        in_specs=[anywhere] * 4 + [smem] + [vmem] * 5,
        out_specs=(vmem, vmem),
        scratch_shapes=[
            pltpu.VMEM((NY, TOK, COLS), bf16),
            pltpu.VMEM((NY, 8, COLS), f32),
            pltpu.VMEM((BLOCKS, WROWS, 2 * HEAD_SIZE), bf16),
            pltpu.VMEM((BLOCKS, WROWS, COLS), bf16),
            pltpu.VMEM((BLOCKS, WROWS, COLS), bf16),
            pltpu.VMEM((BLOCKS, TOK, HEAD_SIZE), bf16),
            pltpu.VMEM((BLOCKS, TOK, HEAD_SIZE), bf16),
            pltpu.VMEM((NY, TOK, COLS), bf16),
            pltpu.VMEM((TOK, 128), f32),
            pltpu.VMEM((2, TOK, 128), f32),
            pltpu.VMEM((NZ, NX * NC * TOK), jnp.int32),
            pltpu.VMEM((GROUP, TOK, HEAD_SIZE), bf16),
            pltpu.VMEM((GROUP, TOK, 128), f32),
            pltpu.VMEM((GROUP, TOK, 128), f32),
            pltpu.VMEM((GROUP, TOK, 128), f32),
            pltpu.VMEM((TOK, COLS), bf16),
            pltpu.VMEM((4, TOK, COLS), bf16),
            pltpu.VMEM((4, TOK, COLS), bf16),
            pltpu.VMEM((4, TOK, COLS), bf16),
            pltpu.VMEM((4, TOK, COLS), bf16),
            pltpu.VMEM((NY, 8, 128), f32),
            dma((4,)),
            dma((8 * HALVES,)),
            dma((8 * HALVES,)),
            dma((NY,)),
            dma((NY,)),
            *gathers,
            dma((4 * SUBS,)),
            dma((4 * SUBS,)),
            dma((4 * SUBS,)),
            dma((4 * SUBS,)),
            dma((NY,)),
            dma((NY,)),
        ],
        compiler_params=pltpu.CompilerParams(
            collective_id=0, has_side_effects=True, vmem_limit_bytes=56 << 20
        ),
    )(
        hidden_in,
        w_query,
        key_value_weight.reshape(WROWS, 2 * HEAD_SIZE),
        w_out.T,
        span_order,
        norm_gain,
        bias_query,
        bias_kv,
        jnp.asarray(inside),
        jnp.asarray(spans),
    )
    stream = hidden_in.astype(f32) + mixed
    normed = stream * scale[:, 0:1] * post_gain.astype(f32)[None, :]
    return mixed.astype(bf16), normed.astype(bf16)


def solution(mesh):
    torus = Mesh(mesh.devices.reshape(NZ, NX, NC, NY), ("z", "x", "c", "y"))
    in_specs = (
        P(SEQ, "y"),
        P(),
        P("y"),
        P(SEQ, "y"),
        P("y"),
        P(SEQ, None, "y"),
        P(None, "y"),
        P("y", SEQ),
        P("y"),
    )
    out_specs = (P(SEQ, "y"), P(SEQ, "y"))
    return jax.shard_map(
        per_device, mesh=torus, in_specs=in_specs, out_specs=out_specs, check_vma=False
    )
```

time: 123 us -> 109 us (0.89)
  the two profiles are of different devices: /device:TPU:2 before, /device:TPU:8 now
where the time goes in v1:
time: 109 us; the launch traced here: 108 us
  Pallas kernels  103 us (94%)
  local copies, waits for them, and re-layouts  3 us (3%)
  other arithmetic  1.78 us (2%)
    pallas_call x1, Pallas kernels, per_device(): pl.pallas_call(kernel, out_shape=(jax.ShapeDtypeStruct((TOK, COLS), f32),...  103 us

profile of v1, /device:TPU:8, one launch (start us, length us, event | category | flops | bytes accessed | tf_op | source)
XLA Modules:
  0.0 108.2 jit_solution(2337129088771052415)
XLA Ops:
  0.6 0.0 copy-start.1
  0.6 0.7 copy-done.1
  1.3 1.4 %copy.15 = bf16[8,8,2,128]{3,1,2,0:T(8,128)(2,1)} copy(bf16[8,8,2,128]{3,2,1,0:T(2,128)(2,1)} %bitcast.7) | data formatting | bytes 65536
  2.7 0.0 copy-start
  2.7 102.8 %shard_map.122 = (f32[128,512]{1,0:T(8,128)}, f32[128,128]{1,0:T(8,128)}) custom-call(bf16[128,512]{1,0:T(8,128)(2,1)} %hidden_ref.1, bf16[64,512]{1,0:T(8,128)(2,1)} %wq_ref.1, bf16[64,256]{1,0:T(8,128)(2,1)} %bitcast.5, bf16[64,512]{1,0:T(8,128)(2,1)} %bitcast.6, s32[64]{0:T(128)} %span_ref.1, bf16[512]{0:T(512)(128)(2,1)} %gain_ref.1, ...), custom_call_target="tpu_custom_call" | custom-call | tf_op jit(solution)/shard_map/pallas_call | solution.py:579
  105.5 0.9 slice_reduce_fusion
  106.4 0.0 copy-done
  106.5 1.8 %multiply_convert_fusion = (bf16[128,512]{1,0:T(8,128)(2,1)}, bf16[128,512]{1,0:T(8,128)(2,1)}) fusion(f32[128,512]{1,0:T(8,128)} %get-tuple-element.4, bf16[128,512]{1,0:T(8,128)(2,1)S(1)} %copy-done, f32[512]{0:T(512)S(1)} %convert_element_type.14, f32[128]{0:T(128)S(1)} %slice_reduce_fusion), kind=kLoop, calls=%fused_computation | loop fusion | flops 393216 | bytes 657920 | tf_op jit(solution)/shard_map/convert_element_type | solution.py:639
  (1 shorter events, 0.0 us)
Async XLA Ops:
  0.6 0.7 copy-start.1
  2.7 103.8 %copy-start = (bf16[128,512]{1,0:T(8,128)(2,1)S(1)}, bf16[128,512]{1,0:T(8,128)(2,1)}, u32[]{:S(2)}) copy-start(bf16[128,512]{1,0:T(8,128)(2,1)} %hidden_ref.1) | copy-start | bytes 393220

commit v2 on v1

--- a/solution.py
+++ b/solution.py
@@ -220,7 +220,7 @@
     u,
     inv,
     rope,
-    kpos,
+    token_gap,
     qs,
     top,
     total,
@@ -293,11 +293,9 @@
     lanes = lax.broadcasted_iota(jnp.int32, (TOK, 128), 1)
     sine = inside_ref[1] * cos_s + inside_ref[0] * sin_s
     rope[1] = jnp.where(lanes < HEAD_SIZE // 2, -sine, sine)
-    token = lax.broadcasted_iota(jnp.int32, (1, TOK), 1)
-    for row in range(NZ):
-        for k in range(NX * NC):
-            where = slice(k * TOK, (k + 1) * TOK)
-            kpos[row : row + 1, where] = token + span_ref[row * NX * NC + k] * TOK
+    key_token = lax.broadcasted_iota(jnp.int32, (TOK, COLS), 0)
+    query_token = lax.rem(lax.broadcasted_iota(jnp.int32, (TOK, COLS), 1), TOK)
+    token_gap[...] = key_token - query_token
     inv[...] = jnp.zeros_like(inv)
     pl.semaphore_wait(barrier, len(friends))
 
@@ -362,51 +360,57 @@
         keys = pair[:, :HEAD_SIZE] * scale + bkv_ref[0:1, :].astype(jnp.float32)
         values = pair[:, HEAD_SIZE:] * scale + bkv_ref[1:2, :].astype(jnp.float32)
         ks[me] = rotate(keys).astype(jnp.bfloat16)
-        vs[me] = values.astype(jnp.bfloat16)
+        vs[me] = values.T.astype(jnp.bfloat16)
 
     def make_query():
         query = project(wq, COLS)
         bias = bq_ref[...].astype(jnp.float32).reshape(1, COLS)
         for g in range(GROUP):
             lanes = slice(g * HEAD_SIZE, (g + 1) * HEAD_SIZE)
-            qs[g] = rotate(query[:, lanes] * inv[...] + bias[:, lanes]).astype(jnp.bfloat16)
+            one = rotate(query[:, lanes] * inv[...] + bias[:, lanes])
+            qs[g * TOK : (g + 1) * TOK, :] = one.astype(jnp.bfloat16)
 
     def attend(row):
         first = row == 0
-        seq_row = lax.rem(z - row + NZ, NZ)
-        chunk = NX * NC * TOK
-        query_pos = lax.broadcasted_iota(jnp.int32, (TOK, 128), 0) + own_span * TOK
-
-        def head(g, carry):
-            scores = lax.dot_general(
-                qs[g],
-                ks[pl.ds(seq_row * NX * NC, NX * NC)].reshape(chunk, HEAD_SIZE),
-                (((1,), (1,)), ((), ())),
-                preferred_element_type=jnp.float32,
-            )
-            allowed = kpos[pl.ds(seq_row, 1), :] <= query_pos[:, 0:1]
-            scores = jnp.where(allowed, scores * exponent_scale, -1e30)
-            peak = jnp.max(scores, axis=1, keepdims=True)
-            if not first:
-                old = top[g][:, 0:1]
-                peak = jnp.maximum(old, peak)
-            weights = jnp.exp2(scores - peak)
-            count = jnp.sum(weights, axis=1, keepdims=True)
-            summed = jnp.dot(
-                weights.astype(jnp.bfloat16),
-                vs[pl.ds(seq_row * NX * NC, NX * NC)].reshape(chunk, HEAD_SIZE),
-                preferred_element_type=jnp.float32,
-            )
-            if not first:
-                factor = jnp.exp2(old - peak)
-                count = count + total[g][:, 0:1] * factor
-                summed = summed + acc[g] * factor
-            top[g] = jnp.broadcast_to(peak, (TOK, 128))
-            total[g] = jnp.broadcast_to(count, (TOK, 128))
-            acc[g] = summed
-            return carry
-
-        lax.fori_loop(0, GROUP, head, 0)
+        base = lax.rem(z - row + NZ, NZ) * NX * NC
+        count = NX * NC
+        keys = ks[pl.ds(base, count)].reshape(count * TOK, HEAD_SIZE)
+        scores = lax.dot_general(
+            keys, qs[...], (((1,), (1,)), ((), ())), preferred_element_type=jnp.float32
+        )
+        blocks, shifts, peak = [], [], None
+        for k in range(count):
+            block = scores[k * TOK : (k + 1) * TOK] * exponent_scale
+            ahead = own_span - span_ref[base + k]
+            if first:
+                block = jnp.where(token_gap[...] <= ahead * TOK, block, -1e30)
+                shift = jnp.float32(0.0)
+            else:
+                shift = jnp.where(ahead > 0, 0.0, 1e30).astype(jnp.float32)
+            high = jnp.max(block, axis=0, keepdims=True) - shift
+            peak = high if peak is None else jnp.maximum(peak, high)
+            blocks.append(block)
+            shifts.append(shift)
+        if not first:
+            old = top[0:1, :]
+            peak = jnp.maximum(old, peak)
+        weights, sums = [], None
+        for block, shift in zip(blocks, shifts):
+            w = jnp.exp2(block - (peak + shift))
+            part = jnp.sum(w, axis=0, keepdims=True)
+            sums = part if sums is None else sums + part
+            weights.append(w.astype(jnp.bfloat16))
+        values = jnp.concatenate([vs[base + k] for k in range(count)], axis=1)
+        summed = jnp.dot(
+            values, jnp.concatenate(weights, axis=0), preferred_element_type=jnp.float32
+        )
+        if not first:
+            factor = jnp.exp2(old - peak)
+            sums = sums + total[0:1, :] * factor
+            summed = summed + acc[...] * factor
+        top[0:1, :] = peak
+        total[0:1, :] = sums
+        acc[...] = summed
 
     seen_gain = {0}
     for step in planned_steps():
@@ -446,7 +450,9 @@
                 starts[g].wait()
             gathers[g].arrived(o)
     for g in range(GROUP):
-        attended[:, g * HEAD_SIZE : (g + 1) * HEAD_SIZE] = (acc[g] / total[g]).astype(jnp.bfloat16)
+        lanes = slice(g * TOK, (g + 1) * TOK)
+        one = (acc[:, lanes] / total[0:1, lanes]).T
+        attended[:, g * HEAD_SIZE : (g + 1) * HEAD_SIZE] = one.astype(jnp.bfloat16)
     gathers["wo"].wait_handed()
 
     def partial(target):
@@ -595,11 +601,11 @@
             pltpu.VMEM((NY, TOK, COLS), bf16),
             pltpu.VMEM((TOK, 128), f32),
             pltpu.VMEM((2, TOK, 128), f32),
-            pltpu.VMEM((NZ, NX * NC * TOK), jnp.int32),
-            pltpu.VMEM((GROUP, TOK, HEAD_SIZE), bf16),
-            pltpu.VMEM((GROUP, TOK, 128), f32),
-            pltpu.VMEM((GROUP, TOK, 128), f32),
-            pltpu.VMEM((GROUP, TOK, 128), f32),
+            pltpu.VMEM((TOK, COLS), jnp.int32),
+            pltpu.VMEM((COLS, HEAD_SIZE), bf16),
+            pltpu.VMEM((8, COLS), f32),
+            pltpu.VMEM((8, COLS), f32),
+            pltpu.VMEM((HEAD_SIZE, COLS), f32),
             pltpu.VMEM((TOK, COLS), bf16),
             pltpu.VMEM((4, TOK, COLS), bf16),
             pltpu.VMEM((4, TOK, COLS), bf16),

time: 109 us -> 98.8 us (0.906)
  Pallas kernels: 103 us -> 93.1 us
    pallas_call x1, Pallas kernels: 103 us -> 93.1 us  [per_device(): pl.pallas_call(kernel, out_shape=(jax.ShapeDtypeStruct((TOK, COLS), f32),...]
where the time goes in v2:
time: 98.8 us; the launch traced here: 98.6 us
  Pallas kernels  93.1 us (94%)
  local copies, waits for them, and re-layouts  3 us (3%)
  other arithmetic  1.78 us (2%)
    pallas_call x1, Pallas kernels, per_device(): pl.pallas_call(kernel, out_shape=(jax.ShapeDtypeStruct((TOK, COLS), f32),...  93.1 us
    unnamed x5, local copies, waits for them, and re-layouts  2.05 us

profile of v2, /device:TPU:8, one launch (start us, length us, event | category | flops | bytes accessed | tf_op | source)
XLA Modules:
  0.0 98.6 jit_solution(6061797010932375316)
XLA Ops:
  0.6 0.0 copy-start.1
  0.6 0.7 copy-done.1
  1.3 1.4 %copy.15 = bf16[8,8,2,128]{3,1,2,0:T(8,128)(2,1)} copy(bf16[8,8,2,128]{3,2,1,0:T(2,128)(2,1)} %bitcast.7) | data formatting | bytes 65536
  2.7 0.0 copy-start
  2.7 93.1 %shard_map.122 = (f32[128,512]{1,0:T(8,128)}, f32[128,128]{1,0:T(8,128)}) custom-call(bf16[128,512]{1,0:T(8,128)(2,1)} %hidden_ref.1, bf16[64,512]{1,0:T(8,128)(2,1)} %wq_ref.1, bf16[64,256]{1,0:T(8,128)(2,1)} %bitcast.5, bf16[64,512]{1,0:T(8,128)(2,1)} %bitcast.6, s32[64]{0:T(128)} %span_ref.1, bf16[512]{0:T(512)(128)(2,1)} %gain_ref.1, ...), custom_call_target="tpu_custom_call" | custom-call | tf_op jit(solution)/shard_map/pallas_call | solution.py:585
  95.8 0.9 slice_reduce_fusion
  96.8 0.0 copy-done
  96.8 1.8 %multiply_convert_fusion = (bf16[128,512]{1,0:T(8,128)(2,1)}, bf16[128,512]{1,0:T(8,128)(2,1)}) fusion(f32[128,512]{1,0:T(8,128)} %get-tuple-element.4, bf16[128,512]{1,0:T(8,128)(2,1)S(1)} %copy-done, f32[512]{0:T(512)S(1)} %convert_element_type.14, f32[128]{0:T(128)S(1)} %slice_reduce_fusion), kind=kLoop, calls=%fused_computation | loop fusion | flops 393216 | bytes 657920 | tf_op jit(solution)/shard_map/convert_element_type | solution.py:645
  (1 shorter events, 0.0 us)
Async XLA Ops:
  0.6 0.7 copy-start.1
  2.7 94.1 %copy-start = (bf16[128,512]{1,0:T(8,128)(2,1)S(1)}, bf16[128,512]{1,0:T(8,128)(2,1)}, u32[]{:S(2)}) copy-start(bf16[128,512]{1,0:T(8,128)(2,1)} %hidden_ref.1) | copy-start | bytes 393220

commit v3 on v2

--- a/solution.py
+++ b/solution.py
@@ -198,18 +198,27 @@
 
 
 def kernel(
-    hidden_ref,
-    wq_ref,
-    wkv_ref,
-    wo_ref,
+    hidden_in_hbm,
+    wq_hbm,
+    wkv_hbm,
+    wo_hbm,
+    span_hbm,
+    gain_hbm,
+    bq_hbm,
+    bkv_hbm,
+    post_hbm,
+    inside_hbm,
+    spans_hbm,
+    mixed_ref,
+    normed_ref,
+    pair_weight,
     span_ref,
     gain_ref,
     bq_ref,
     bkv_ref,
+    post_ref,
     inside_ref,
     spans_ref,
-    mixed_ref,
-    scale_ref,
     hid,
     gains,
     wkv,
@@ -275,15 +284,28 @@
     friends += [(z, x, c, lax.rem(y + d, NY)) for d in range(1, NY)]
     for f in friends:
         pl.semaphore_signal(barrier, inc=1, device_id=f, device_id_type=MESH_ID)
-    starts = {
-        "wkv": pltpu.make_async_copy(wkv_ref, wkv.at[me], local_sem.at[0]),
-        "hid": pltpu.make_async_copy(hidden_ref, hid.at[y], local_sem.at[1]),
-        "wq": pltpu.make_async_copy(wq_ref, wq.at[me], local_sem.at[2]),
-        "wo": pltpu.make_async_copy(wo_ref, wo.at[me], local_sem.at[3]),
-    }
-    for s in starts.values():
-        s.start()
-
+    starts = {}
+    for name, src, dst in (
+        ("wkv", wkv_hbm, pair_weight),
+        ("span", span_hbm, span_ref),
+        ("gain", gain_hbm, gain_ref),
+        ("inside", inside_hbm, inside_ref),
+        ("spans", spans_hbm, spans_ref),
+        ("hid", hidden_in_hbm, hid.at[y]),
+        ("wq", wq_hbm, wq.at[me]),
+        ("bkv", bkv_hbm, bkv_ref),
+        ("bq", bq_hbm, bq_ref),
+        ("wo", wo_hbm, wo.at[me]),
+        ("post", post_hbm, post_ref),
+    ):
+        starts[name] = pltpu.make_async_copy(src, dst, local_sem.at[len(starts)])
+        starts[name].start()
+
+    starts["wkv"].wait()
+    wkv[me, :, 0:HEAD_SIZE] = pair_weight[:, 0, :]
+    wkv[me, :, HEAD_SIZE : 2 * HEAD_SIZE] = pair_weight[:, 1, :]
+    for name in ("span", "gain", "inside", "spans", "bkv", "bq", "post"):
+        starts[name].wait()
     own_gain = gain_ref[...].astype(jnp.float32).reshape(1, COLS)
     gains[y] = jnp.broadcast_to(own_gain, (8, COLS))
     own_span = span_ref[me]
@@ -446,7 +468,7 @@
             attend(step[1])
         else:
             g, o = step
-            if o == (0, 0) and g in starts:
+            if o == (0, 0) and g in ("wq", "wo"):
                 starts[g].wait()
             gathers[g].arrived(o)
     for g in range(GROUP):
@@ -551,7 +573,12 @@
     for k in range(1, NY):
         summed = summed + stats[k]
     rows = jnp.broadcast_to(summed[0:1, :], (128, TOK)).T
-    scale_ref[...] = lax.rsqrt(rows / MODEL_WIDTH + eps)
+    scale = lax.rsqrt(rows / MODEL_WIDTH + eps)
+    post = post_ref[...].astype(jnp.float32).reshape(1, COLS)
+    for g in range(GROUP):
+        lanes = slice(g * 128, (g + 1) * 128)
+        stream = hid[y, :, lanes].astype(jnp.float32) + mixed_ref[:, lanes]
+        normed_ref[:, lanes] = stream * scale * post[:, lanes]
     for d in range(1, NY):
         stats_copy(d, y).wait_send()
 
@@ -576,21 +603,28 @@
 
     bf16, f32 = jnp.bfloat16, jnp.float32
     vmem = pl.BlockSpec(memory_space=pltpu.VMEM)
-    smem = pl.BlockSpec(memory_space=pltpu.SMEM)
     anywhere = pl.BlockSpec(memory_space=pl.ANY)
     dma = pltpu.SemaphoreType.DMA
     gathers = []
     for rows in (1, 1, 1, NZ, NZ):
         gathers += [dma((PLANE,)), dma((rows,)), dma((1,))]
-    mixed, scale = pl.pallas_call(
+    mixed, normed = pl.pallas_call(
         kernel,
         out_shape=(
             jax.ShapeDtypeStruct((TOK, COLS), f32),
-            jax.ShapeDtypeStruct((TOK, 128), f32),
+            jax.ShapeDtypeStruct((TOK, COLS), f32),
         ),
-        in_specs=[anywhere] * 4 + [smem] + [vmem] * 5,
+        in_specs=[anywhere] * 11,
         out_specs=(vmem, vmem),
         scratch_shapes=[
+            pltpu.VMEM((WROWS, 2, HEAD_SIZE), bf16),
+            pltpu.SMEM((BLOCKS,), jnp.int32),
+            pltpu.VMEM((COLS,), bf16),
+            pltpu.VMEM((COLS,), bf16),
+            pltpu.VMEM((2, HEAD_SIZE), bf16),
+            pltpu.VMEM((COLS,), bf16),
+            pltpu.VMEM((2, TOK, HEAD_SIZE), f32),
+            pltpu.VMEM((BLOCKS, 2, HEAD_SIZE), f32),
             pltpu.VMEM((NY, TOK, COLS), bf16),
             pltpu.VMEM((NY, 8, COLS), f32),
             pltpu.VMEM((BLOCKS, WROWS, 2 * HEAD_SIZE), bf16),
@@ -612,7 +646,7 @@
             pltpu.VMEM((4, TOK, COLS), bf16),
             pltpu.VMEM((4, TOK, COLS), bf16),
             pltpu.VMEM((NY, 8, 128), f32),
-            dma((4,)),
+            dma((11,)),
             dma((8 * HALVES,)),
             dma((8 * HALVES,)),
             dma((NY,)),
@@ -631,17 +665,16 @@
     )(
         hidden_in,
         w_query,
-        key_value_weight.reshape(WROWS, 2 * HEAD_SIZE),
+        key_value_weight,
         w_out.T,
         span_order,
         norm_gain,
         bias_query,
         bias_kv,
+        post_gain,
         jnp.asarray(inside),
         jnp.asarray(spans),
     )
-    stream = hidden_in.astype(f32) + mixed
-    normed = stream * scale[:, 0:1] * post_gain.astype(f32)[None, :]
     return mixed.astype(bf16), normed.astype(bf16)
 
 

time: 98.8 us -> 95.3 us (0.965)
  local copies, waits for them, and re-layouts: 3 us -> 0.01 us
  Pallas kernels: 93.1 us -> 92.1 us
    unnamed x5 -> x2, local copies, waits for them, and re-layouts: 2.05 us -> 0.01 us
    convert_element_type x1 -> x2, other arithmetic: 1.78 us -> 2.34 us  [per_device(): return (mixed.astype(bf16), normed.astype(bf16))]
where the time goes in v3:
time: 95.3 us; the launch traced here: 95.1 us
  Pallas kernels  92.1 us (97%)
  other arithmetic  2.34 us (2%)
    pallas_call x1, Pallas kernels, per_device(): pl.pallas_call(kernel, out_shape=(jax.ShapeDtypeStruct((TOK, COLS), f32),...  92.1 us
    convert_element_type x2, other arithmetic, per_device(): return (mixed.astype(bf16), normed.astype(bf16))  2.34 us

profile of v3, /device:TPU:8, one launch (start us, length us, event | category | flops | bytes accessed | tf_op | source)
XLA Modules:
  0.0 95.1 jit_solution(2499928306936851648)
XLA Ops:
  0.6 92.1 %shard_map.122 = (f32[128,512]{1,0:T(8,128)}, f32[128,512]{1,0:T(8,128)}) custom-call(bf16[128,512]{1,0:T(8,128)(2,1)} %hidden_in_hbm.1, bf16[64,512]{1,0:T(8,128)(2,1)} %wq_hbm.1, bf16[64,2,128]{2,1,0:T(2,128)(2,1)} %wkv_hbm.1, bf16[64,512]{1,0:T(8,128)(2,1)} %bitcast.1, s32[64]{0:T(128)} %span_hbm.1, bf16[512]{0:T(512)(128)(2,1)} %gain_hbm.1, ...), custom_call_target="tpu_custom_call" | custom-call | tf_op jit(solution)/shard_map/pallas_call | solution.py:611
  92.8 0.0 copy-start
  92.8 1.7 %convert_element_type.6 = bf16[128,512]{1,0:T(8,128)(2,1)} convert(f32[128,512]{1,0:T(8,128)} %get-tuple-element.4) | non-fusion elementwise | flops 65536 | bytes 393216 | tf_op jit(solution)/shard_map/convert_element_type | solution.py:678
  94.5 0.0 copy-done
  94.5 0.7 convert_element_type.7
Async XLA Ops:
  92.8 1.7 %copy-start = (f32[128,512]{1,0:T(8,128)S(1)}, f32[128,512]{1,0:T(8,128)}, u32[]{:S(2)}) copy-start(f32[128,512]{1,0:T(8,128)} %get-tuple-element.5) | copy-start | bytes 786436

commit v4 on v3

--- a/solution.py
+++ b/solution.py
@@ -28,8 +28,8 @@
 rope_base = 1000000.0
 exponent_scale = math.log2(math.e) / math.sqrt(HEAD_SIZE)
 
-RATE, HOP, FURTHER, HOP_Y, HAND = 46.6, 3.3, 0.7, 2.1, 1.6
-WO_START = 12.0
+RATE, HOP, FURTHER, HOP_Y, HAND = 46.6, 2.2, 0.7, 2.1, 1.6
+WQ_START, WO_START = 0.0, 0.0
 
 
 def x_then_z(direct_x):
@@ -54,12 +54,19 @@
     return parent
 
 
+def mirrored(tree):
+    def turn(o):
+        return (o[0] if o[0] == NX // 2 else -o[0], o[1] if o[1] == NZ // 2 else -o[1])
+
+    return {turn(child): turn(parent) for child, parent in tree.items()}
+
+
 TREES = {
-    "wkv": z_then_x(4),
-    "wq": x_then_z(True),
-    "wo": z_then_x(1),
-    "k": z_then_x(2),
-    "v": x_then_z(False),
+    "wkv": mirrored(z_then_x(3)),
+    "wq": mirrored(z_then_x(1)),
+    "wo": mirrored(x_then_z(True)),
+    "k": mirrored(x_then_z(True)),
+    "v": mirrored(z_then_x(2)),
 }
 KB = {"wkv": 32, "wq": 64, "wo": 64, "k": 32, "v": 32}
 
@@ -82,7 +89,7 @@
     free, heap, steps = {}, [], []
     got, tail = dict.fromkeys(TREES, 0), dict.fromkeys(TREES, 0.0)
     rows_in, waiting = {}, []
-    now, hidden_left = 0.0, 6 * HALVES + 2
+    now, hidden_left = 0.0, 7 * HALVES
     keys_done = query_done = own_row_done = False
 
     def push(t, *what):
@@ -96,7 +103,7 @@
         return end + latency + FURTHER * (hops - 1)
 
     push(0.0, "wkv", (0, 0))
-    push(0.0, "wq", (0, 0))
+    push(WQ_START, "wq", (0, 0))
     push(WO_START, "wo", (0, 0))
     for piece in range(HALVES):
         for sign in (1, -1):
@@ -132,7 +139,7 @@
             if hop:
                 hidden_left -= 1
                 now += 0.25 / HALVES
-            if hop < 3 or (hop == 3 and piece == (sign < 0)):
+            if hop < 3 or (hop == 3 and (piece < HALVES // 2) == (sign > 0)):
                 route = [("y+" if sign > 0 else "y-", 1)]
                 kb = TOK / HALVES
                 push(transfer(route, kb, HOP_Y), "hid", hop + 1, sign, piece)
@@ -209,8 +216,8 @@
     post_hbm,
     inside_hbm,
     spans_hbm,
+    both_ref,
     mixed_ref,
-    normed_ref,
     pair_weight,
     span_ref,
     gain_ref,
@@ -348,7 +355,7 @@
         return remote(block, block, hid_sent.at[k], hid_arrive.at[k], y_near(sign))
 
     def hid_goes(hop, sign, piece):
-        return hop < 3 or (hop == 3 and piece == (sign < 0))
+        return hop < 3 or (hop == 3 and (piece < HALVES // 2) == (sign > 0))
 
     def gain_copy(d, source):
         block = gains.at[source]
@@ -369,7 +376,8 @@
             block = weights[pl.ds(k * (BLOCKS // NY), BLOCKS // NY)].reshape(COLS, width)
             return total + jnp.dot(u[k], block, preferred_element_type=jnp.float32)
 
-        return lax.fori_loop(0, NY, step, jnp.zeros((TOK, width), jnp.float32))
+        zero = jnp.zeros((TOK, width), jnp.float32)
+        return lax.fori_loop(0, NY, step, zero, unroll=True)
 
     def rotate(head):
         return head * rope[0] + pltpu.roll(head, HEAD_SIZE // 2, 1) * rope[1]
@@ -540,6 +548,7 @@
             + minus_in[3, rows].astype(jnp.float32)
         )
         mixed_ref[rows, :] = mixed
+        both_ref[0, rows, :] = mixed.astype(jnp.bfloat16)
         stream = hid[y, rows].astype(jnp.float32) + mixed
         squares = stream * stream
         part = squares[:, 0:128]
@@ -578,7 +587,7 @@
     for g in range(GROUP):
         lanes = slice(g * 128, (g + 1) * 128)
         stream = hid[y, :, lanes].astype(jnp.float32) + mixed_ref[:, lanes]
-        normed_ref[:, lanes] = stream * scale * post[:, lanes]
+        both_ref[1, :, lanes] = (stream * scale * post[:, lanes]).astype(jnp.bfloat16)
     for d in range(1, NY):
         stats_copy(d, y).wait_send()
 
@@ -608,15 +617,13 @@
     gathers = []
     for rows in (1, 1, 1, NZ, NZ):
         gathers += [dma((PLANE,)), dma((rows,)), dma((1,))]
-    mixed, normed = pl.pallas_call(
+    both = pl.pallas_call(
         kernel,
-        out_shape=(
-            jax.ShapeDtypeStruct((TOK, COLS), f32),
-            jax.ShapeDtypeStruct((TOK, COLS), f32),
-        ),
+        out_shape=jax.ShapeDtypeStruct((2, TOK, COLS), bf16),
         in_specs=[anywhere] * 11,
-        out_specs=(vmem, vmem),
+        out_specs=vmem,
         scratch_shapes=[
+            pltpu.VMEM((TOK, COLS), f32),
             pltpu.VMEM((WROWS, 2, HEAD_SIZE), bf16),
             pltpu.SMEM((BLOCKS,), jnp.int32),
             pltpu.VMEM((COLS,), bf16),
@@ -675,7 +682,7 @@
         jnp.asarray(inside),
         jnp.asarray(spans),
     )
-    return mixed.astype(bf16), normed.astype(bf16)
+    return both[0], both[1]
 
 
 def solution(mesh):

time: 95.3 us -> 92.1 us (0.966)
  Pallas kernels: 92.1 us -> 89.6 us
  other arithmetic: 2.34 us -> 0 us
  local copies, waits for them, and re-layouts: 0.01 us -> 1.68 us
    pallas_call x1, Pallas kernels: 92.1 us -> 89.6 us  [per_device(): pl.pallas_call(kernel, out_shape=jax.ShapeDtypeStruct((2, TOK, COLS), bf1...]
    convert_element_type x2 -> x0, other arithmetic: 2.34 us -> none  [per_device(): return (mixed.astype(bf16), normed.astype(bf16))]
    squeeze x0 -> x1, local copies, waits for them, and re-layouts: none -> 1.68 us  [per_device(): return (both[0], both[1])]
where the time goes in v4:
time: 92.1 us; the launch traced here: 91.9 us
  Pallas kernels  89.6 us (97%)
  local copies, waits for them, and re-layouts  1.68 us (2%)
    pallas_call x1, Pallas kernels, per_device(): pl.pallas_call(kernel, out_shape=jax.ShapeDtypeStruct((2, TOK, COLS), bf1...  89.6 us

profile of v4, /device:TPU:8, one launch (start us, length us, event | category | flops | bytes accessed | tf_op | source)
XLA Modules:
  0.0 91.9 jit_solution(2612996458400151353)
XLA Ops:
  0.6 89.6 %shard_map.122 = bf16[2,128,512]{2,1,0:T(8,128)(2,1)} custom-call(bf16[128,512]{1,0:T(8,128)(2,1)} %hidden_in_hbm.1, bf16[64,512]{1,0:T(8,128)(2,1)} %wq_hbm.1, bf16[64,2,128]{2,1,0:T(2,128)(2,1)} %wkv_hbm.1, bf16[64,512]{1,0:T(8,128)(2,1)} %bitcast.5, s32[64]{0:T(128)} %span_hbm.1, bf16[512]{0:T(512)(128)(2,1)} %gain_hbm.1, bf16[512]{0:T(512)(128)(2,1)} %bq_hbm.1, ...), custom_call_target="tpu_custom_call" | custom-call | tf_op jit(solution)/shard_map/pallas_call | solution.py:620
  90.2 1.7 %slice_bitcast_fusion = (bf16[128,512]{1,0:T(8,128)(2,1)}, bf16[128,512]{1,0:T(8,128)(2,1)}) fusion(bf16[2,128,512]{2,1,0:T(8,128)(2,1)} %shard_map.122), kind=kLoop, calls=%fused_computation | loop fusion | bytes 524288 | tf_op jit(solution)/shard_map/squeeze | solution.py:685

commit v5 on v4

--- a/solution.py
+++ b/solution.py
@@ -113,19 +113,19 @@
         keys_at = max(now, tail["wkv"] + HAND)
         query_at = max(now, tail["wq"] + HAND)
         if not keys_done and got["wkv"] == PLANE and not hidden_left and ahead >= keys_at - 0.3:
-            now, keys_done = keys_at + 1.8, True
+            now, keys_done = keys_at + 1.1, True
             steps.append(("keys",))
             push(now, "k", (0, 0))
             push(now + 0.01, "v", (0, 0))
             continue
         if keys_done and not query_done and got["wq"] == PLANE and ahead >= query_at - 0.3:
-            now, query_done = query_at + 2.5, True
+            now, query_done = query_at + 1.5, True
             steps.append(("query",))
             continue
         able = [w for w in waiting if own_row_done or w[1] == 0]
         if query_done and able and ahead >= max(now, able[0][0]) - 0.2:
             waiting.remove(able[0])
-            now = max(now, able[0][0]) + 0.9
+            now = max(now, able[0][0]) + 0.7
             own_row_done = True
             steps.append(("attend", able[0][1]))
             continue

time: 92.1 us -> 92 us (level)
  no operation moved by 1% of the time
where the time goes in v5:
time: 92 us; the launch traced here: 91.9 us
  Pallas kernels  89.5 us (97%)
  local copies, waits for them, and re-layouts  1.68 us (2%)
    pallas_call x1, Pallas kernels, per_device(): pl.pallas_call(kernel, out_shape=jax.ShapeDtypeStruct((2, TOK, COLS), bf1...  89.5 us

profile of v5, /device:TPU:8, one launch (start us, length us, event | category | flops | bytes accessed | tf_op | source)
XLA Modules:
  0.0 91.9 jit_solution(3233093061740473398)
XLA Ops:
  0.6 89.5 %shard_map.122 = bf16[2,128,512]{2,1,0:T(8,128)(2,1)} custom-call(bf16[128,512]{1,0:T(8,128)(2,1)} %hidden_in_hbm.1, bf16[64,512]{1,0:T(8,128)(2,1)} %wq_hbm.1, bf16[64,2,128]{2,1,0:T(2,128)(2,1)} %wkv_hbm.1, bf16[64,512]{1,0:T(8,128)(2,1)} %bitcast.5, s32[64]{0:T(128)} %span_hbm.1, bf16[512]{0:T(512)(128)(2,1)} %gain_hbm.1, bf16[512]{0:T(512)(128)(2,1)} %bq_hbm.1, ...), custom_call_target="tpu_custom_call" | custom-call | tf_op jit(solution)/shard_map/pallas_call | solution.py:620
  90.2 1.7 %slice_bitcast_fusion = (bf16[128,512]{1,0:T(8,128)(2,1)}, bf16[128,512]{1,0:T(8,128)(2,1)}) fusion(bf16[2,128,512]{2,1,0:T(8,128)(2,1)} %shard_map.122), kind=kLoop, calls=%fused_computation | loop fusion | bytes 524288 | tf_op jit(solution)/shard_map/squeeze | solution.py:685
